TPU v7x, 256 devices: a whole 4x4x8 slice. The times are simulated.
256 devices in a mesh: section: 8 (over x, core), expert: 32 (over z, y).
Axes of the slice: x: 4, y: 4, z: 8, core: 2. Of those that a mesh axis runs over, the one named last changes fastest.
Arguments:
- tokens: bfloat16 [4, 1024, 2048], P(None, 'expert'), may hold values from -6 to 6
- attn_norm: float32 [8, 2048], P('section'), may hold values from 0.5 to 2
- moe_norm: float32 [8, 2048], P('section'), may hold values from 0.5 to 2
- query_weight: bfloat16 [8, 2048, 1024], P('section', 'expert'), may hold values from -4 to 4
- key_weight: bfloat16 [8, 2048, 128], P('section', 'expert'), may hold values from -0.125 to 0.125
- value_weight: bfloat16 [8, 2048, 128], P('section', 'expert'), may hold values from -0.125 to 0.125
- out_weight: bfloat16 [8, 1024, 2048], P('section', 'expert'), may hold values from -0.1875 to 0.1875
- gate_proj: bfloat16 [8, 32, 2048, 704], P('section', 'expert'), may hold values from -0.125 to 0.125
- up_proj: bfloat16 [8, 32, 2048, 704], P('section', 'expert'), may hold values from -0.125 to 0.125
- down_proj: bfloat16 [8, 32, 704, 2048], P('section', 'expert'), may hold values from -0.21875 to 0.21875
- routes: int32 [8, 4, 1024, 6], P('section', None, 'expert'), may hold values from 0 to 31, all different within a row; in each aligned block of 32 rows (0 to 31, 32 to 63, ..., all dimensions but the last counted through in order) at most 8 rows name the same one
- weights_code: int32 [8, 4, 1024, 6], P('section', None, 'expert'), may hold values from 8 to 64
Outputs:
- hidden_states: bfloat16 [8, 4, 1024, 2048], P('section', None, 'expert')
Inputs may be any that keep to these rules, and one draw needn't show every extreme that they name: `routes`: each row names 6 different experts. In each aligned block of 32 rows (one sequence's tokens of one micro-batch of one layer) no expert is named by more than 8 rows, a bound that some block reaches.
All inputs are finite; a program needn't handle non-finite values.
Results may differ from a plain program's by a relative error of at most 0.03.
Values may be sent and summed in bfloat16 or wider, within the bound.
No kernel may reach another device: no remote copies, remote signals or barrier semaphores. Data moves between devices by JAX's collectives and lax.ppermute only.
A program may use at most 128 MiB of HBM per device.

v0:
```python
import jax
import jax.numpy as jnp
from jax import lax
from jax.sharding import PartitionSpec as P

epsilon = 1e-06


def shifted(value, axis, steps):
    count = lax.axis_size(axis)
    initial, last = (max(0, -steps), min(count, count - steps))
    return lax.ppermute(value, axis, [(source, source + steps) for source in range(initial, last)])


def rms_scale(features, gain_vector):
    return (
        features
        * lax.rsqrt(jnp.mean(features * features, axis=-1, keepdims=True) + epsilon)
        * gain_vector
    )


def expert_rows(slot_rows, gate_matrix, up_matrix, down_matrix):
    gated = jnp.dot(slot_rows, gate_matrix, preferred_element_type=jnp.float32)
    lifted = jnp.dot(slot_rows, up_matrix, preferred_element_type=jnp.float32)
    hidden = (jax.nn.silu(gated) * lifted).astype(jnp.bfloat16)
    return jnp.dot(hidden, down_matrix, preferred_element_type=jnp.float32).astype(jnp.bfloat16)


def route_tables(picks_block, codes_block, expert_count, capacity):
    tok_rows, pick_count = picks_block.shape
    flat_ids = picks_block.reshape(-1)
    matches = (flat_ids[:, None] == jnp.arange(expert_count, dtype=jnp.int32)[None, :]).astype(
        jnp.int32
    )
    slot_ranks = jnp.sum((jnp.cumsum(matches, axis=0) - matches) * matches, axis=1)
    columns = flat_ids * capacity + slot_ranks
    onehot = (
        columns[:, None] == jnp.arange(expert_count * capacity, dtype=jnp.int32)[None, :]
    ).astype(jnp.float32)
    onehot = onehot.reshape(tok_rows, pick_count, expert_count * capacity)
    scatter_table = jnp.sum(onehot, axis=1).astype(jnp.bfloat16)
    pick_weights = codes_block.astype(jnp.float32) / 64.0
    combine_table = jnp.sum(onehot * pick_weights[:, :, None], axis=1).astype(jnp.bfloat16)
    return (scatter_table, combine_table)


def shards(
    tokens,
    attn_norm,
    moe_norm,
    query_weight,
    key_weight,
    value_weight,
    out_weight,
    gate_proj,
    up_proj,
    down_proj,
    routes,
    weights_code,
):
    section_count = lax.axis_size("section")
    section_index = lax.axis_index("section")
    expert_devices = lax.axis_size("expert")
    micro_count, tok_rows, model_width = tokens.shape
    pick_count = routes.shape[3]
    expert_count = expert_devices * gate_proj.shape[1]
    capacity = min(tok_rows, tok_rows * pick_count * 4 // (3 * expert_count))
    full_query, full_key, full_value, full_out = (
        lax.all_gather(query_weight, "expert", axis=1, tiled=True),
        lax.all_gather(key_weight, "expert", axis=1, tiled=True),
        lax.all_gather(value_weight, "expert", axis=1, tiled=True),
        lax.all_gather(out_weight, "expert", axis=1, tiled=True),
    )
    full_query = full_query[0]
    full_key = full_key[0]
    full_value = full_value[0]
    full_out = full_out[0]
    head_size = full_key.shape[-1]
    head_count = full_query.shape[-1] // head_size
    length = micro_count * tok_rows
    score_scale = head_size ** (-0.5)
    attn_gain = attn_norm[0]
    moe_gain = moe_norm[0]
    gate_matrix = gate_proj[0, 0]
    up_matrix = up_proj[0, 0]
    down_matrix = down_proj[0, 0]
    route_layer = routes[0]
    code_layer = weights_code[0]

    def feed_rows(slot_rows):
        return expert_rows(slot_rows, gate_matrix, up_matrix, down_matrix)

    def blank_rows(slot_rows):
        return jnp.zeros((slot_rows.shape[0], model_width), jnp.bfloat16)

    def advance(tick_index, state_carry):
        inbound, key_cache, value_cache, stored = state_carry
        block_index = tick_index - section_index
        active = (block_index >= 0) & (block_index < micro_count)
        clipped = jnp.clip(block_index, 0, micro_count - 1)
        first_rows = lax.dynamic_index_in_dim(tokens, clipped, 0, keepdims=False)
        layer_input = jnp.where(section_index == 0, first_rows, inbound)
        picks_block = lax.dynamic_index_in_dim(route_layer, clipped, 0, keepdims=False)
        codes_block = lax.dynamic_index_in_dim(code_layer, clipped, 0, keepdims=False)
        scatter_table, combine_table = route_tables(
            picks_block, codes_block, expert_count, capacity
        )
        wide_input = layer_input.astype(jnp.float32)
        moe_input = rms_scale(wide_input, moe_gain).astype(jnp.bfloat16)

        def attend(caches):
            old_keys, old_values = caches
            normed = rms_scale(wide_input, attn_gain).astype(jnp.bfloat16)
            query_rows = jnp.dot(normed, full_query, preferred_element_type=jnp.float32).astype(
                jnp.bfloat16
            )
            query_rows = query_rows.reshape(tok_rows, head_count, head_size)
            new_keys = jnp.dot(normed, full_key, preferred_element_type=jnp.float32).astype(
                jnp.bfloat16
            )
            new_values = jnp.dot(normed, full_value, preferred_element_type=jnp.float32).astype(
                jnp.bfloat16
            )
            offset = clipped * tok_rows
            key_vectors = lax.dynamic_update_slice_in_dim(old_keys, new_keys, offset, 0)
            value_vectors = lax.dynamic_update_slice_in_dim(old_values, new_values, offset, 0)
            attention_scores = (
                jnp.einsum(
                    "qhd,kd->hqk", query_rows, key_vectors, preferred_element_type=jnp.float32
                )
                * score_scale
            )
            positions = offset + jnp.arange(tok_rows, dtype=jnp.int32)
            causal = jnp.arange(length, dtype=jnp.int32)[None, :] <= positions[:, None]
            attention_scores = jnp.where(causal[None], attention_scores, -1e30)
            highest = jnp.max(attention_scores, axis=-1, keepdims=True)
            exponent = jnp.exp(attention_scores - highest)
            attention_probabilities = (exponent / jnp.sum(exponent, axis=-1, keepdims=True)).astype(
                jnp.bfloat16
            )
            attended_values = jnp.einsum(
                "hqk,kd->qhd",
                attention_probabilities,
                value_vectors,
                preferred_element_type=jnp.float32,
            )
            attended_values = attended_values.astype(jnp.bfloat16).reshape(
                tok_rows, head_count * head_size
            )
            attended = jnp.dot(attended_values, full_out, preferred_element_type=jnp.float32)
            return (attended, key_vectors, value_vectors)

        def skipped(caches):
            return (jnp.zeros((tok_rows, model_width), jnp.float32), caches[0], caches[1])

        attended, key_cache, value_cache = lax.cond(
            active, attend, skipped, (key_cache, value_cache)
        )
        outgoing = jnp.einsum(
            "te,td->ed", scatter_table, moe_input, preferred_element_type=jnp.float32
        )
        outgoing = outgoing.astype(jnp.bfloat16).reshape(expert_count, capacity, model_width)
        arrived = lax.all_to_all(outgoing, "expert", split_axis=0, concat_axis=0, tiled=True)
        slot_rows = arrived.reshape(-1, model_width)
        produced = lax.cond(active, feed_rows, blank_rows, slot_rows).reshape(arrived.shape)
        returned = lax.all_to_all(produced, "expert", split_axis=0, concat_axis=0, tiled=True)
        mixed = jnp.dot(
            combine_table, returned.reshape(-1, model_width), preferred_element_type=jnp.float32
        )
        output_rows = (wide_input + attended + mixed).astype(jnp.bfloat16)
        updated = lax.dynamic_update_index_in_dim(stored, output_rows, clipped, 0)
        stored = jnp.where(active, updated, stored)
        inbound = shifted(output_rows, "section", 1)
        return (inbound, key_cache, value_cache, stored)

    initial = (
        jnp.zeros((tok_rows, model_width), jnp.bfloat16),
        jnp.zeros((length, head_size), jnp.bfloat16),
        jnp.zeros((length, head_size), jnp.bfloat16),
        jnp.zeros((micro_count, tok_rows, model_width), jnp.bfloat16),
    )
    finals = lax.fori_loop(0, micro_count + section_count - 1, advance, initial)
    return finals[3][None]


def solution(mesh):
    placed = (
        P(None, "expert", None),
        P("section", None),
        P("section", None),
        P("section", "expert", None),
        P("section", "expert", None),
        P("section", "expert", None),
        P("section", "expert", None),
        P("section", "expert", None, None),
        P("section", "expert", None, None),
        P("section", "expert", None, None),
        P("section", None, "expert", None),
        P("section", None, "expert", None),
    )
    return jax.shard_map(
        shards,
        mesh=mesh,
        in_specs=placed,
        out_specs=P("section", None, "expert", None),
        check_vma=False,
    )
```

profile of v0, /device:TPU:10, one launch (start us, length us, event | category | flops | bytes accessed | tf_op | source)
XLA Modules:
  0.0 1040.3 jit_solution(5070451524895726768)
XLA Ops:
  17.4 52.8 %all_gather.13 = bf16[1,2048,128]{2,1,0:T(8,128)(2,1)S(1)} all-gather(bf16[1,64,128]{2,1,0:T(8,128)(2,1)S(1)} %copy-done.3), channel_id=1, replica_groups=mesh['section'=8,'expert'=32] {'expert'}, dimensions={1}, use_global_device_ids=true | all-gather | bytes 540672 | tf_op jit(solution)/shard_map/all_gather | solution.py:71
  70.1 47.8 %all_gather.12 = bf16[1,2048,128]{2,1,0:T(8,128)(2,1)S(1)} all-gather(bf16[1,64,128]{2,1,0:T(8,128)(2,1)S(1)} %copy-done.4), channel_id=1, replica_groups=mesh['section'=8,'expert'=32] {'expert'}, dimensions={1}, use_global_device_ids=true | all-gather | bytes 540672 | tf_op jit(solution)/shard_map/all_gather | solution.py:72
  118.0 57.3 %all-gather.5.cloned.1.call-done = bf16[1,1024,2048]{2,1,0:T(8,128)(2,1)} async-done(((bf16[1,32,2048]{2,1,0:T(8,128)(2,1)}), bf16[1,1024,2048]{2,1,0:T(8,128)(2,1)}) %all-gather.5.cloned.1.call-update) | async-done | bytes 4194320 | tf_op jit(solution)/shard_map/all_gather | solution.py:73
  175.4 857.3 %while.20 = (s32[]{:T(128)}, bf16[32,2048]{1,0:T(8,128)(2,1)S(1)}, bf16[128,128]{1,0:T(8,128)(2,1)S(1)}, bf16[128,128]{1,0:T(8,128)(2,1)S(1)}, bf16[4,32,2048]{2...) while((s32[]{:T(128)}, bf16[32,2048]{1,0:T(8,128)(2,1)S(1)}, ...), condition=%wide.region_14.15_spmd, body=%wide.region_0.14_spmd.sunk | while | flops 2613929216 | bytes 35623652 | solution.py:183
  186.4 25.4 %all-to-all-done = bf16[32,8,2048]{2,1,0:T(8,128)(2,1)S(1)} async-done(((bf16[32,8,2048]{2,1,0:T(8,128)(2,1)}), bf16[32,8,2048]{2,1,0:T(8,128)(2,1)S(1)}, u32[]{:S(2)}, u32[]{:S(2)}) %all-to-all-start) | async-done | bytes 1048608 | tf_op jit(solution)/shard_map/while/body/eval_jaxpr/all_to_all | solution.py:164
  218.6 25.2 %all-to-all-done.1 = bf16[32,8,2048]{2,1,0:T(8,128)(2,1)S(1)} async-done(((bf16[32,8,2048]{2,1,0:T(8,128)(2,1)}), bf16[32,8,2048]{2,1,0:T(8,128)(2,1)S(1)}, u32[]{:S(2)}, u32[]{:S(2)}) %all-to-all-start.1) | async-done | bytes 1048608 | tf_op jit(solution)/shard_map/while/body/eval_jaxpr/all_to_all | solution.py:167
  260.0 27.3 %all-to-all-done = bf16[32,8,2048]{2,1,0:T(8,128)(2,1)S(1)} async-done(((bf16[32,8,2048]{2,1,0:T(8,128)(2,1)}), bf16[32,8,2048]{2,1,0:T(8,128)(2,1)S(1)}, u32[]{:S(2)}, u32[]{:S(2)}) %all-to-all-start) | async-done | bytes 1048608 | tf_op jit(solution)/shard_map/while/body/eval_jaxpr/all_to_all | solution.py:164
  294.1 26.7 %all-to-all-done.1 = bf16[32,8,2048]{2,1,0:T(8,128)(2,1)S(1)} async-done(((bf16[32,8,2048]{2,1,0:T(8,128)(2,1)}), bf16[32,8,2048]{2,1,0:T(8,128)(2,1)S(1)}, u32[]{:S(2)}, u32[]{:S(2)}) %all-to-all-start.1) | async-done | bytes 1048608 | tf_op jit(solution)/shard_map/while/body/eval_jaxpr/all_to_all | solution.py:167
  323.1 11.2 %collective-permute-done = bf16[32,2048]{1,0:T(8,128)(2,1)S(1)} collective-permute-done((bf16[32,2048]{1,0:T(8,128)(2,1)S(1)}, bf16[32,2048]{1,0:T(8,128)(2,1)S(1)}, u32[]{:S(2)}, u32[]{:S(2)}) %collective-permute-start) | collective-permute-done | bytes 131104 | tf_op jit(solution)/shard_map/while/body/eval_jaxpr/ppermute | solution.py:12
  345.0 19.0 %all-to-all-done = bf16[32,8,2048]{2,1,0:T(8,128)(2,1)S(1)} async-done(((bf16[32,8,2048]{2,1,0:T(8,128)(2,1)}), bf16[32,8,2048]{2,1,0:T(8,128)(2,1)S(1)}, u32[]{:S(2)}, u32[]{:S(2)}) %all-to-all-start) | async-done | bytes 1048608 | tf_op jit(solution)/shard_map/while/body/eval_jaxpr/all_to_all | solution.py:164
  364.0 11.4 %conditional.4 = (bf16[256,2048]{1,0:T(8,128)(2,1)}) conditional(s32[]{:T(128)} %convert_element_type.170, () %tuple.60, (bf16[32,8,2048]{2,1,0:T(8,128)(2,1)S(1)}, bf16[2048,704]{1,0:T(8,128)(2,1)}, bf16[2048,704]{1,0:T(8,128)(2,1)}, bf16[704,2048]{1,0:T(8,128)(2,1)}) %tuple.61), branch_computations={%region_12.12_spmd, %region_13.13_spmd} | conditional | flops 2216198144 | bytes 13238280 | solution.py:166
  401.4 17.6 %collective-permute-done = bf16[32,2048]{1,0:T(8,128)(2,1)S(1)} collective-permute-done((bf16[32,2048]{1,0:T(8,128)(2,1)S(1)}, bf16[32,2048]{1,0:T(8,128)(2,1)S(1)}, u32[]{:S(2)}, u32[]{:S(2)}) %collective-permute-start) | collective-permute-done | bytes 131104 | tf_op jit(solution)/shard_map/while/body/eval_jaxpr/ppermute | solution.py:12
  429.8 18.2 %all-to-all-done = bf16[32,8,2048]{2,1,0:T(8,128)(2,1)S(1)} async-done(((bf16[32,8,2048]{2,1,0:T(8,128)(2,1)}), bf16[32,8,2048]{2,1,0:T(8,128)(2,1)S(1)}, u32[]{:S(2)}, u32[]{:S(2)}) %all-to-all-start) | async-done | bytes 1048608 | tf_op jit(solution)/shard_map/while/body/eval_jaxpr/all_to_all | solution.py:164
  448.1 11.4 %conditional.4 = (bf16[256,2048]{1,0:T(8,128)(2,1)}) conditional(s32[]{:T(128)} %convert_element_type.170, () %tuple.60, (bf16[32,8,2048]{2,1,0:T(8,128)(2,1)S(1)}, bf16[2048,704]{1,0:T(8,128)(2,1)}, bf16[2048,704]{1,0:T(8,128)(2,1)}, bf16[704,2048]{1,0:T(8,128)(2,1)}) %tuple.61), branch_computations={%region_12.12_spmd, %region_13.13_spmd} | conditional | flops 2216198144 | bytes 13238280 | solution.py:166
  485.5 18.4 %collective-permute-done = bf16[32,2048]{1,0:T(8,128)(2,1)S(1)} collective-permute-done((bf16[32,2048]{1,0:T(8,128)(2,1)S(1)}, bf16[32,2048]{1,0:T(8,128)(2,1)S(1)}, u32[]{:S(2)}, u32[]{:S(2)}) %collective-permute-start) | collective-permute-done | bytes 131104 | tf_op jit(solution)/shard_map/while/body/eval_jaxpr/ppermute | solution.py:12
  514.7 18.2 %all-to-all-done = bf16[32,8,2048]{2,1,0:T(8,128)(2,1)S(1)} async-done(((bf16[32,8,2048]{2,1,0:T(8,128)(2,1)}), bf16[32,8,2048]{2,1,0:T(8,128)(2,1)S(1)}, u32[]{:S(2)}, u32[]{:S(2)}) %all-to-all-start) | async-done | bytes 1048608 | tf_op jit(solution)/shard_map/while/body/eval_jaxpr/all_to_all | solution.py:164
  532.9 11.4 %conditional.4 = (bf16[256,2048]{1,0:T(8,128)(2,1)}) conditional(s32[]{:T(128)} %convert_element_type.170, () %tuple.60, (bf16[32,8,2048]{2,1,0:T(8,128)(2,1)S(1)}, bf16[2048,704]{1,0:T(8,128)(2,1)}, bf16[2048,704]{1,0:T(8,128)(2,1)}, bf16[704,2048]{1,0:T(8,128)(2,1)}) %tuple.61), branch_computations={%region_12.12_spmd, %region_13.13_spmd} | conditional | flops 2216198144 | bytes 13238280 | solution.py:166
  570.3 13.0 %collective-permute-done = bf16[32,2048]{1,0:T(8,128)(2,1)S(1)} collective-permute-done((bf16[32,2048]{1,0:T(8,128)(2,1)S(1)}, bf16[32,2048]{1,0:T(8,128)(2,1)S(1)}, u32[]{:S(2)}, u32[]{:S(2)}) %collective-permute-start) | collective-permute-done | bytes 131104 | tf_op jit(solution)/shard_map/while/body/eval_jaxpr/ppermute | solution.py:12
  593.0 18.2 %all-to-all-done = bf16[32,8,2048]{2,1,0:T(8,128)(2,1)S(1)} async-done(((bf16[32,8,2048]{2,1,0:T(8,128)(2,1)}), bf16[32,8,2048]{2,1,0:T(8,128)(2,1)S(1)}, u32[]{:S(2)}, u32[]{:S(2)}) %all-to-all-start) | async-done | bytes 1048608 | tf_op jit(solution)/shard_map/while/body/eval_jaxpr/all_to_all | solution.py:164
  611.2 11.4 %conditional.4 = (bf16[256,2048]{1,0:T(8,128)(2,1)}) conditional(s32[]{:T(128)} %convert_element_type.170, () %tuple.60, (bf16[32,8,2048]{2,1,0:T(8,128)(2,1)S(1)}, bf16[2048,704]{1,0:T(8,128)(2,1)}, bf16[2048,704]{1,0:T(8,128)(2,1)}, bf16[704,2048]{1,0:T(8,128)(2,1)}) %tuple.61), branch_computations={%region_12.12_spmd, %region_13.13_spmd} | conditional | flops 2216198144 | bytes 13238280 | solution.py:166
  667.9 19.5 %all-to-all-done = bf16[32,8,2048]{2,1,0:T(8,128)(2,1)S(1)} async-done(((bf16[32,8,2048]{2,1,0:T(8,128)(2,1)}), bf16[32,8,2048]{2,1,0:T(8,128)(2,1)S(1)}, u32[]{:S(2)}, u32[]{:S(2)}) %all-to-all-start) | async-done | bytes 1048608 | tf_op jit(solution)/shard_map/while/body/eval_jaxpr/all_to_all | solution.py:164
  694.5 28.7 %all-to-all-done.1 = bf16[32,8,2048]{2,1,0:T(8,128)(2,1)S(1)} async-done(((bf16[32,8,2048]{2,1,0:T(8,128)(2,1)}), bf16[32,8,2048]{2,1,0:T(8,128)(2,1)S(1)}, u32[]{:S(2)}, u32[]{:S(2)}) %all-to-all-start.1) | async-done | bytes 1048608 | tf_op jit(solution)/shard_map/while/body/eval_jaxpr/all_to_all | solution.py:167
  742.4 23.4 %all-to-all-done = bf16[32,8,2048]{2,1,0:T(8,128)(2,1)S(1)} async-done(((bf16[32,8,2048]{2,1,0:T(8,128)(2,1)}), bf16[32,8,2048]{2,1,0:T(8,128)(2,1)S(1)}, u32[]{:S(2)}, u32[]{:S(2)}) %all-to-all-start) | async-done | bytes 1048608 | tf_op jit(solution)/shard_map/while/body/eval_jaxpr/all_to_all | solution.py:164
  772.5 23.7 %all-to-all-done.1 = bf16[32,8,2048]{2,1,0:T(8,128)(2,1)S(1)} async-done(((bf16[32,8,2048]{2,1,0:T(8,128)(2,1)}), bf16[32,8,2048]{2,1,0:T(8,128)(2,1)S(1)}, u32[]{:S(2)}, u32[]{:S(2)}) %all-to-all-start.1) | async-done | bytes 1048608 | tf_op jit(solution)/shard_map/while/body/eval_jaxpr/all_to_all | solution.py:167
  816.9 22.2 %all-to-all-done = bf16[32,8,2048]{2,1,0:T(8,128)(2,1)S(1)} async-done(((bf16[32,8,2048]{2,1,0:T(8,128)(2,1)}), bf16[32,8,2048]{2,1,0:T(8,128)(2,1)S(1)}, u32[]{:S(2)}, u32[]{:S(2)}) %all-to-all-start) | async-done | bytes 1048608 | tf_op jit(solution)/shard_map/while/body/eval_jaxpr/all_to_all | solution.py:164
  845.8 22.3 %all-to-all-done.1 = bf16[32,8,2048]{2,1,0:T(8,128)(2,1)S(1)} async-done(((bf16[32,8,2048]{2,1,0:T(8,128)(2,1)}), bf16[32,8,2048]{2,1,0:T(8,128)(2,1)S(1)}, u32[]{:S(2)}, u32[]{:S(2)}) %all-to-all-start.1) | async-done | bytes 1048608 | tf_op jit(solution)/shard_map/while/body/eval_jaxpr/all_to_all | solution.py:167
  870.4 10.4 collective-permute-done
  891.5 21.1 %all-to-all-done = bf16[32,8,2048]{2,1,0:T(8,128)(2,1)S(1)} async-done(((bf16[32,8,2048]{2,1,0:T(8,128)(2,1)}), bf16[32,8,2048]{2,1,0:T(8,128)(2,1)S(1)}, u32[]{:S(2)}, u32[]{:S(2)}) %all-to-all-start) | async-done | bytes 1048608 | tf_op jit(solution)/shard_map/while/body/eval_jaxpr/all_to_all | solution.py:164
  919.3 20.8 %all-to-all-done.1 = bf16[32,8,2048]{2,1,0:T(8,128)(2,1)S(1)} async-done(((bf16[32,8,2048]{2,1,0:T(8,128)(2,1)}), bf16[32,8,2048]{2,1,0:T(8,128)(2,1)S(1)}, u32[]{:S(2)}, u32[]{:S(2)}) %all-to-all-start.1) | async-done | bytes 1048608 | tf_op jit(solution)/shard_map/while/body/eval_jaxpr/all_to_all | solution.py:167
  942.3 13.0 %collective-permute-done = bf16[32,2048]{1,0:T(8,128)(2,1)S(1)} collective-permute-done((bf16[32,2048]{1,0:T(8,128)(2,1)S(1)}, bf16[32,2048]{1,0:T(8,128)(2,1)S(1)}, u32[]{:S(2)}, u32[]{:S(2)}) %collective-permute-start) | collective-permute-done | bytes 131104 | tf_op jit(solution)/shard_map/while/body/eval_jaxpr/ppermute | solution.py:12
  966.0 26.8 %all-to-all-done = bf16[32,8,2048]{2,1,0:T(8,128)(2,1)S(1)} async-done(((bf16[32,8,2048]{2,1,0:T(8,128)(2,1)}), bf16[32,8,2048]{2,1,0:T(8,128)(2,1)S(1)}, u32[]{:S(2)}, u32[]{:S(2)}) %all-to-all-start) | async-done | bytes 1048608 | tf_op jit(solution)/shard_map/while/body/eval_jaxpr/all_to_all | solution.py:164
  999.6 26.4 %all-to-all-done.1 = bf16[32,8,2048]{2,1,0:T(8,128)(2,1)S(1)} async-done(((bf16[32,8,2048]{2,1,0:T(8,128)(2,1)}), bf16[32,8,2048]{2,1,0:T(8,128)(2,1)S(1)}, u32[]{:S(2)}, u32[]{:S(2)}) %all-to-all-start.1) | async-done | bytes 1048608 | tf_op jit(solution)/shard_map/while/body/eval_jaxpr/all_to_all | solution.py:167
  (387 shorter events, 410.0 us)
Async XLA Ops:
  6.5 111.5 %all-gather.3.cloned.1.call-start = ((), (), s32[]{:S(2)}) async-start(), calls=%async_computation.2 | async-start | bytes 4325376 | tf_op jit(solution)/shard_map/all_gather | solution.py:70
  7.3 168.0 %all-gather.5.cloned.1.call-start = ((), (), s32[]{:S(2)}) async-start(), calls=%async_computation.3 | async-start | bytes 4325376 | tf_op jit(solution)/shard_map/all_gather | solution.py:73
  179.5 32.4 %all-to-all-start = ((bf16[32,8,2048]{2,1,0:T(8,128)(2,1)}), bf16[32,8,2048]{2,1,0:T(8,128)(2,1)S(1)}, u32[]{:S(2)}, u32[]{:S(2)}) async-start(bf16[32,8,2048]{2,1,0:T(8,128)(2,1)} %fusion.71), calls=%async_computation | async-start | bytes 2097152 | tf_op jit(solution)/shard_map/while/body/eval_jaxpr/all_to_all | solution.py:164
  213.0 30.8 %all-to-all-start.1 = ((bf16[32,8,2048]{2,1,0:T(8,128)(2,1)}), bf16[32,8,2048]{2,1,0:T(8,128)(2,1)S(1)}, u32[]{:S(2)}, u32[]{:S(2)}) async-start(bf16[32,8,2048]{2,1,0:T(8,128)(2,1)} %bitcast.125), calls=%async_computation.1 | async-start | bytes 2097152 | tf_op jit(solution)/shard_map/while/body/eval_jaxpr/all_to_all | solution.py:167
  254.4 32.9 %all-to-all-start = ((bf16[32,8,2048]{2,1,0:T(8,128)(2,1)}), bf16[32,8,2048]{2,1,0:T(8,128)(2,1)S(1)}, u32[]{:S(2)}, u32[]{:S(2)}) async-start(bf16[32,8,2048]{2,1,0:T(8,128)(2,1)} %fusion.71), calls=%async_computation | async-start | bytes 2097152 | tf_op jit(solution)/shard_map/while/body/eval_jaxpr/all_to_all | solution.py:164
  288.5 32.4 %all-to-all-start.1 = ((bf16[32,8,2048]{2,1,0:T(8,128)(2,1)}), bf16[32,8,2048]{2,1,0:T(8,128)(2,1)S(1)}, u32[]{:S(2)}, u32[]{:S(2)}) async-start(bf16[32,8,2048]{2,1,0:T(8,128)(2,1)} %bitcast.125), calls=%async_computation.1 | async-start | bytes 2097152 | tf_op jit(solution)/shard_map/while/body/eval_jaxpr/all_to_all | solution.py:167
  321.1 13.1 %collective-permute-start = (bf16[32,2048]{1,0:T(8,128)(2,1)S(1)}, bf16[32,2048]{1,0:T(8,128)(2,1)S(1)}, u32[]{:S(2)}, u32[]{:S(2)}) collective-permute-start(bf16[32,2048]{1,0:T(8,128)(2,1)S(1)} %get-tuple-element.610), channel_id=1, source_target_pairs={{0,32},{32,64},{64,96},{96,128},{128,160},{160,192},{192,224},{1,3... | collective-permute-start | bytes 393224 | tf_op jit(solution)/shard_map/while/body/eval_jaxpr/ppermute | solution.py:12
  338.3 25.7 %all-to-all-start = ((bf16[32,8,2048]{2,1,0:T(8,128)(2,1)}), bf16[32,8,2048]{2,1,0:T(8,128)(2,1)S(1)}, u32[]{:S(2)}, u32[]{:S(2)}) async-start(bf16[32,8,2048]{2,1,0:T(8,128)(2,1)} %fusion.71), calls=%async_computation | async-start | bytes 2097152 | tf_op jit(solution)/shard_map/while/body/eval_jaxpr/all_to_all | solution.py:164
  375.4 23.8 %all-to-all-start.1 = ((bf16[32,8,2048]{2,1,0:T(8,128)(2,1)}), bf16[32,8,2048]{2,1,0:T(8,128)(2,1)S(1)}, u32[]{:S(2)}, u32[]{:S(2)}) async-start(bf16[32,8,2048]{2,1,0:T(8,128)(2,1)} %bitcast.125), calls=%async_computation.1 | async-start | bytes 2097152 | tf_op jit(solution)/shard_map/while/body/eval_jaxpr/all_to_all | solution.py:167
  399.5 19.6 %collective-permute-start = (bf16[32,2048]{1,0:T(8,128)(2,1)S(1)}, bf16[32,2048]{1,0:T(8,128)(2,1)S(1)}, u32[]{:S(2)}, u32[]{:S(2)}) collective-permute-start(bf16[32,2048]{1,0:T(8,128)(2,1)S(1)} %get-tuple-element.610), channel_id=1, source_target_pairs={{0,32},{32,64},{64,96},{96,128},{128,160},{160,192},{192,224},{1,3... | collective-permute-start | bytes 393224 | tf_op jit(solution)/shard_map/while/body/eval_jaxpr/ppermute | solution.py:12
  423.1 24.9 %all-to-all-start = ((bf16[32,8,2048]{2,1,0:T(8,128)(2,1)}), bf16[32,8,2048]{2,1,0:T(8,128)(2,1)S(1)}, u32[]{:S(2)}, u32[]{:S(2)}) async-start(bf16[32,8,2048]{2,1,0:T(8,128)(2,1)} %fusion.71), calls=%async_computation | async-start | bytes 2097152 | tf_op jit(solution)/shard_map/while/body/eval_jaxpr/all_to_all | solution.py:164
  459.5 23.8 %all-to-all-start.1 = ((bf16[32,8,2048]{2,1,0:T(8,128)(2,1)}), bf16[32,8,2048]{2,1,0:T(8,128)(2,1)S(1)}, u32[]{:S(2)}, u32[]{:S(2)}) async-start(bf16[32,8,2048]{2,1,0:T(8,128)(2,1)} %bitcast.125), calls=%async_computation.1 | async-start | bytes 2097152 | tf_op jit(solution)/shard_map/while/body/eval_jaxpr/all_to_all | solution.py:167
  483.6 20.3 %collective-permute-start = (bf16[32,2048]{1,0:T(8,128)(2,1)S(1)}, bf16[32,2048]{1,0:T(8,128)(2,1)S(1)}, u32[]{:S(2)}, u32[]{:S(2)}) collective-permute-start(bf16[32,2048]{1,0:T(8,128)(2,1)S(1)} %get-tuple-element.610), channel_id=1, source_target_pairs={{0,32},{32,64},{64,96},{96,128},{128,160},{160,192},{192,224},{1,3... | collective-permute-start | bytes 393224 | tf_op jit(solution)/shard_map/while/body/eval_jaxpr/ppermute | solution.py:12
  508.0 24.9 %all-to-all-start = ((bf16[32,8,2048]{2,1,0:T(8,128)(2,1)}), bf16[32,8,2048]{2,1,0:T(8,128)(2,1)S(1)}, u32[]{:S(2)}, u32[]{:S(2)}) async-start(bf16[32,8,2048]{2,1,0:T(8,128)(2,1)} %fusion.71), calls=%async_computation | async-start | bytes 2097152 | tf_op jit(solution)/shard_map/while/body/eval_jaxpr/all_to_all | solution.py:164
  544.3 23.8 %all-to-all-start.1 = ((bf16[32,8,2048]{2,1,0:T(8,128)(2,1)}), bf16[32,8,2048]{2,1,0:T(8,128)(2,1)S(1)}, u32[]{:S(2)}, u32[]{:S(2)}) async-start(bf16[32,8,2048]{2,1,0:T(8,128)(2,1)} %bitcast.125), calls=%async_computation.1 | async-start | bytes 2097152 | tf_op jit(solution)/shard_map/while/body/eval_jaxpr/all_to_all | solution.py:167
  568.4 14.9 %collective-permute-start = (bf16[32,2048]{1,0:T(8,128)(2,1)S(1)}, bf16[32,2048]{1,0:T(8,128)(2,1)S(1)}, u32[]{:S(2)}, u32[]{:S(2)}) collective-permute-start(bf16[32,2048]{1,0:T(8,128)(2,1)S(1)} %get-tuple-element.610), channel_id=1, source_target_pairs={{0,32},{32,64},{64,96},{96,128},{128,160},{160,192},{192,224},{1,3... | collective-permute-start | bytes 393224 | tf_op jit(solution)/shard_map/while/body/eval_jaxpr/ppermute | solution.py:12
  587.4 23.8 %all-to-all-start = ((bf16[32,8,2048]{2,1,0:T(8,128)(2,1)}), bf16[32,8,2048]{2,1,0:T(8,128)(2,1)S(1)}, u32[]{:S(2)}, u32[]{:S(2)}) async-start(bf16[32,8,2048]{2,1,0:T(8,128)(2,1)} %fusion.71), calls=%async_computation | async-start | bytes 2097152 | tf_op jit(solution)/shard_map/while/body/eval_jaxpr/all_to_all | solution.py:164
  622.6 23.8 %all-to-all-start.1 = ((bf16[32,8,2048]{2,1,0:T(8,128)(2,1)}), bf16[32,8,2048]{2,1,0:T(8,128)(2,1)S(1)}, u32[]{:S(2)}, u32[]{:S(2)}) async-start(bf16[32,8,2048]{2,1,0:T(8,128)(2,1)} %bitcast.125), calls=%async_computation.1 | async-start | bytes 2097152 | tf_op jit(solution)/shard_map/while/body/eval_jaxpr/all_to_all | solution.py:167
  646.7 10.7 %collective-permute-start = (bf16[32,2048]{1,0:T(8,128)(2,1)S(1)}, bf16[32,2048]{1,0:T(8,128)(2,1)S(1)}, u32[]{:S(2)}, u32[]{:S(2)}) collective-permute-start(bf16[32,2048]{1,0:T(8,128)(2,1)S(1)} %get-tuple-element.610), channel_id=1, source_target_pairs={{0,32},{32,64},{64,96},{96,128},{128,160},{160,192},{192,224},{1,3... | collective-permute-start | bytes 393224 | tf_op jit(solution)/shard_map/while/body/eval_jaxpr/ppermute | solution.py:12
  661.5 26.0 %all-to-all-start = ((bf16[32,8,2048]{2,1,0:T(8,128)(2,1)}), bf16[32,8,2048]{2,1,0:T(8,128)(2,1)S(1)}, u32[]{:S(2)}, u32[]{:S(2)}) async-start(bf16[32,8,2048]{2,1,0:T(8,128)(2,1)} %fusion.71), calls=%async_computation | async-start | bytes 2097152 | tf_op jit(solution)/shard_map/while/body/eval_jaxpr/all_to_all | solution.py:164
  688.6 34.7 %all-to-all-start.1 = ((bf16[32,8,2048]{2,1,0:T(8,128)(2,1)}), bf16[32,8,2048]{2,1,0:T(8,128)(2,1)S(1)}, u32[]{:S(2)}, u32[]{:S(2)}) async-start(bf16[32,8,2048]{2,1,0:T(8,128)(2,1)} %bitcast.125), calls=%async_computation.1 | async-start | bytes 2097152 | tf_op jit(solution)/shard_map/while/body/eval_jaxpr/all_to_all | solution.py:167
  735.7 30.1 %all-to-all-start = ((bf16[32,8,2048]{2,1,0:T(8,128)(2,1)}), bf16[32,8,2048]{2,1,0:T(8,128)(2,1)S(1)}, u32[]{:S(2)}, u32[]{:S(2)}) async-start(bf16[32,8,2048]{2,1,0:T(8,128)(2,1)} %fusion.71), calls=%async_computation | async-start | bytes 2097152 | tf_op jit(solution)/shard_map/while/body/eval_jaxpr/all_to_all | solution.py:164
  766.9 29.4 %all-to-all-start.1 = ((bf16[32,8,2048]{2,1,0:T(8,128)(2,1)}), bf16[32,8,2048]{2,1,0:T(8,128)(2,1)S(1)}, u32[]{:S(2)}, u32[]{:S(2)}) async-start(bf16[32,8,2048]{2,1,0:T(8,128)(2,1)} %bitcast.125), calls=%async_computation.1 | async-start | bytes 2097152 | tf_op jit(solution)/shard_map/while/body/eval_jaxpr/all_to_all | solution.py:167
  796.6 9.6 collective-permute-start
  810.2 28.9 %all-to-all-start = ((bf16[32,8,2048]{2,1,0:T(8,128)(2,1)}), bf16[32,8,2048]{2,1,0:T(8,128)(2,1)S(1)}, u32[]{:S(2)}, u32[]{:S(2)}) async-start(bf16[32,8,2048]{2,1,0:T(8,128)(2,1)} %fusion.71), calls=%async_computation | async-start | bytes 2097152 | tf_op jit(solution)/shard_map/while/body/eval_jaxpr/all_to_all | solution.py:164
  840.2 27.9 %all-to-all-start.1 = ((bf16[32,8,2048]{2,1,0:T(8,128)(2,1)}), bf16[32,8,2048]{2,1,0:T(8,128)(2,1)S(1)}, u32[]{:S(2)}, u32[]{:S(2)}) async-start(bf16[32,8,2048]{2,1,0:T(8,128)(2,1)} %bitcast.125), calls=%async_computation.1 | async-start | bytes 2097152 | tf_op jit(solution)/shard_map/while/body/eval_jaxpr/all_to_all | solution.py:167
  868.4 12.3 %collective-permute-start = (bf16[32,2048]{1,0:T(8,128)(2,1)S(1)}, bf16[32,2048]{1,0:T(8,128)(2,1)S(1)}, u32[]{:S(2)}, u32[]{:S(2)}) collective-permute-start(bf16[32,2048]{1,0:T(8,128)(2,1)S(1)} %get-tuple-element.610), channel_id=1, source_target_pairs={{0,32},{32,64},{64,96},{96,128},{128,160},{160,192},{192,224},{1,3... | collective-permute-start | bytes 393224 | tf_op jit(solution)/shard_map/while/body/eval_jaxpr/ppermute | solution.py:12
  884.8 27.8 %all-to-all-start = ((bf16[32,8,2048]{2,1,0:T(8,128)(2,1)}), bf16[32,8,2048]{2,1,0:T(8,128)(2,1)S(1)}, u32[]{:S(2)}, u32[]{:S(2)}) async-start(bf16[32,8,2048]{2,1,0:T(8,128)(2,1)} %fusion.71), calls=%async_computation | async-start | bytes 2097152 | tf_op jit(solution)/shard_map/while/body/eval_jaxpr/all_to_all | solution.py:164
  913.7 26.4 %all-to-all-start.1 = ((bf16[32,8,2048]{2,1,0:T(8,128)(2,1)}), bf16[32,8,2048]{2,1,0:T(8,128)(2,1)S(1)}, u32[]{:S(2)}, u32[]{:S(2)}) async-start(bf16[32,8,2048]{2,1,0:T(8,128)(2,1)} %bitcast.125), calls=%async_computation.1 | async-start | bytes 2097152 | tf_op jit(solution)/shard_map/while/body/eval_jaxpr/all_to_all | solution.py:167
  940.3 14.9 %collective-permute-start = (bf16[32,2048]{1,0:T(8,128)(2,1)S(1)}, bf16[32,2048]{1,0:T(8,128)(2,1)S(1)}, u32[]{:S(2)}, u32[]{:S(2)}) collective-permute-start(bf16[32,2048]{1,0:T(8,128)(2,1)S(1)} %get-tuple-element.610), channel_id=1, source_target_pairs={{0,32},{32,64},{64,96},{96,128},{128,160},{160,192},{192,224},{1,3... | collective-permute-start | bytes 393224 | tf_op jit(solution)/shard_map/while/body/eval_jaxpr/ppermute | solution.py:12
  959.3 33.5 %all-to-all-start = ((bf16[32,8,2048]{2,1,0:T(8,128)(2,1)}), bf16[32,8,2048]{2,1,0:T(8,128)(2,1)S(1)}, u32[]{:S(2)}, u32[]{:S(2)}) async-start(bf16[32,8,2048]{2,1,0:T(8,128)(2,1)} %fusion.71), calls=%async_computation | async-start | bytes 2097152 | tf_op jit(solution)/shard_map/while/body/eval_jaxpr/all_to_all | solution.py:164
  994.0 32.1 %all-to-all-start.1 = ((bf16[32,8,2048]{2,1,0:T(8,128)(2,1)}), bf16[32,8,2048]{2,1,0:T(8,128)(2,1)S(1)}, u32[]{:S(2)}, u32[]{:S(2)}) async-start(bf16[32,8,2048]{2,1,0:T(8,128)(2,1)} %bitcast.125), calls=%async_computation.1 | async-start | bytes 2097152 | tf_op jit(solution)/shard_map/while/body/eval_jaxpr/all_to_all | solution.py:167
  (10 other events, 619.5 us)
Sparse Core Ops, SparseCore 0:
  9.9 83.9 all-gather.2
  96.5 78.7 all-gather.4
where the time goes:
time: 1040 us
  waiting for transfers between devices  628 us (60%)
  starting transfers between devices  155 us (15%)
  blocking collectives  101 us (10%)
  matrix products  94.8 us (9%)
  local copies, waits for them, and re-layouts  24.2 us (2%)
  other arithmetic  23.1 us (2%)
  between operations  13.5 us (1%)
    all_to_all x11, waiting for transfers between devices, advance(): lax.all_to_all(outgoing, 'expert', split_axis=0, concat_axis=0, tiled=True)  240 us
    all_to_all x11, waiting for transfers between devices, advance(): lax.all_to_all(produced, 'expert', split_axis=0, concat_axis=0, tiled=True)  215 us
    ppermute x11, waiting for transfers between devices, shifted(): lax.ppermute(value, axis, [(source, source + steps) for source in range(i...  114 us
    all_to_all x11, starting transfers between devices, advance(): lax.all_to_all(outgoing, 'expert', split_axis=0, concat_axis=0, tiled=True)  71.3 us
    all_to_all x11, starting transfers between devices, advance(): lax.all_to_all(produced, 'expert', split_axis=0, concat_axis=0, tiled=True)  61.6 us
    all_gather x1, waiting for transfers between devices, shards(): lax.all_gather(out_weight, 'expert', axis=1, tiled=True)  57.3 us
    all_gather x1, blocking collectives, shards(): lax.all_gather(key_weight, 'expert', axis=1, tiled=True)  52.8 us
    all_gather x1, blocking collectives, shards(): lax.all_gather(value_weight, 'expert', axis=1, tiled=True)  47.8 us
  transfers between devices with their start and end apart: 35, of which 34 were waited for; matrix products, arithmetic and copies ran while one was open for 4% of the time, Pallas kernels for 0%

commit v1 on v0

--- a/solution.py
+++ b/solution.py
@@ -2,6 +2,7 @@
 import jax.numpy as jnp
 from jax import lax
 from jax.sharding import PartitionSpec as P
+from jax.lax import all_to_all, axis_size
 
 epsilon = 1e-06
 
@@ -66,9 +67,16 @@
     pick_count = routes.shape[3]
     expert_count = expert_devices * gate_proj.shape[1]
     capacity = min(tok_rows, tok_rows * pick_count * 4 // (3 * expert_count))
+
+    def lead_ends_on(mine_x):
+        block_now = jnp.concatenate(
+            all_to_all(jnp.stack(axis_size("expert") * [mine_x], 0), "expert", 0, 0), 1
+        )
+        return block_now
+
     full_query, full_key, full_value, full_out = (
         lax.all_gather(query_weight, "expert", axis=1, tiled=True),
-        lax.all_gather(key_weight, "expert", axis=1, tiled=True),
+        lead_ends_on(key_weight),
         lax.all_gather(value_weight, "expert", axis=1, tiled=True),
         lax.all_gather(out_weight, "expert", axis=1, tiled=True),
     )

time: 1040 us -> 1040 us (level)
  blocking collectives: 101 us -> 50 us
  waiting for transfers between devices: 628 us -> 667 us
  starting transfers between devices: 155 us -> 166 us
    all_gather x1 -> x0, blocking collectives: 52.8 us -> none  [shards(): lax.all_gather(key_weight, 'expert', axis=1, tiled=True)]
    all_gather x1, waiting for transfers between devices: 57.3 us -> 81.1 us  [shards(): lax.all_gather(out_weight, 'expert', axis=1, tiled=True)]
    all_gather x1, waiting for transfers between devices: 0.02 us -> 15.6 us  [shards(): lax.all_gather(query_weight, 'expert', axis=1, tiled=True)]
    all_to_all x0 -> x1, starting transfers between devices: none -> 11.7 us  [lead_ends_on(): all_to_all(jnp.stack(axis_size('expert') * [mine_x], 0), 'expert', 0, 0)]
  transfers between devices with their start and end apart: 35 -> 36, of which waited for: 34 -> 35; matrix products, arithmetic and copies ran while one was open for 4% -> 4% of each run, Pallas kernels for 0% -> 0%
where the time goes in v1:
time: 1040 us
  waiting for transfers between devices  667 us (64%)
  starting transfers between devices  166 us (16%)
  matrix products  94.8 us (9%)
  blocking collectives  50 us (5%)
  local copies, waits for them, and re-layouts  24.2 us (2%)
  other arithmetic  23.1 us (2%)
  between operations  13.5 us (1%)
    all_to_all x11, waiting for transfers between devices, advance(): lax.all_to_all(outgoing, 'expert', split_axis=0, concat_axis=0, tiled=True)  240 us
    all_to_all x11, waiting for transfers between devices, advance(): lax.all_to_all(produced, 'expert', split_axis=0, concat_axis=0, tiled=True)  215 us
    ppermute x11, waiting for transfers between devices, shifted(): lax.ppermute(value, axis, [(source, source + steps) for source in range(i...  114 us
    all_gather x1, waiting for transfers between devices, shards(): lax.all_gather(out_weight, 'expert', axis=1, tiled=True)  81.1 us
    all_to_all x11, starting transfers between devices, advance(): lax.all_to_all(outgoing, 'expert', split_axis=0, concat_axis=0, tiled=True)  71.3 us
    all_to_all x11, starting transfers between devices, advance(): lax.all_to_all(produced, 'expert', split_axis=0, concat_axis=0, tiled=True)  61.5 us
    all_gather x1, blocking collectives, shards(): lax.all_gather(value_weight, 'expert', axis=1, tiled=True)  50 us
    dot_general x4, matrix products, expert_rows(): jnp.dot(hidden, down_matrix, preferred_element_type=jnp.float32)  29.1 us
  transfers between devices with their start and end apart: 36, of which 35 were waited for; matrix products, arithmetic and copies ran while one was open for 4% of the time, Pallas kernels for 0%

profile of v1, /device:TPU:10, one launch (start us, length us, event | category | flops | bytes accessed | tf_op | source)
XLA Modules:
  0.0 1040.8 jit_solution(5640849065574281905)
XLA Ops:
  9.6 11.7 %all-to-all-start.2 = ((bf16[32,1,64,128]{3,2,1,0:T(8,128)(2,1)}), bf16[32,1,64,128]{3,2,1,0:T(8,128)(2,1)S(1)}, u32[]{:S(2)}, u32[]{:S(2)}) async-start(bf16[32,1,64,128]{3,2,1,0:T(8,128)(2,1)} %stack.2), calls=%async_computation.2 | async-start | bytes 1048576 | tf_op jit(solution)/shard_map/all_to_all | solution.py:73
  29.0 50.0 %all_gather.9 = bf16[1,2048,128]{2,1,0:T(8,128)(2,1)S(1)} all-gather(bf16[1,64,128]{2,1,0:T(8,128)(2,1)S(1)} %copy-done.4), channel_id=1, replica_groups=mesh['section'=8,'expert'=32] {'expert'}, dimensions={1}, use_global_device_ids=true | all-gather | bytes 540672 | tf_op jit(solution)/shard_map/all_gather | solution.py:80
  79.1 15.6 %all-gather.3.cloned.1.call-done = bf16[1,2048,1024]{2,1,0:T(8,128)(2,1)} async-done(((bf16[1,64,1024]{2,1,0:T(8,128)(2,1)}), bf16[1,2048,1024]{2,1,0:T(8,128)(2,1)}) %all-gather.3.cloned.1.call-update) | async-done | bytes 4194320 | tf_op jit(solution)/shard_map/all_gather | solution.py:78
  94.7 81.1 %all-gather.5.cloned.1.call-done = bf16[1,1024,2048]{2,1,0:T(8,128)(2,1)} async-done(((bf16[1,32,2048]{2,1,0:T(8,128)(2,1)}), bf16[1,1024,2048]{2,1,0:T(8,128)(2,1)}) %all-gather.5.cloned.1.call-update) | async-done | bytes 4194320 | tf_op jit(solution)/shard_map/all_gather | solution.py:81
  175.9 857.2 %while.20 = (s32[]{:T(128)}, bf16[32,2048]{1,0:T(8,128)(2,1)S(1)}, bf16[128,128]{1,0:T(8,128)(2,1)S(1)}, bf16[128,128]{1,0:T(8,128)(2,1)S(1)}, bf16[4,32,2048]{2...) while((s32[]{:T(128)}, bf16[32,2048]{1,0:T(8,128)(2,1)S(1)}, ...), condition=%wide.region_14.15_spmd, body=%wide.region_0.14_spmd.sunk | while | flops 2613929216 | bytes 35623652 | solution.py:191
  187.0 25.4 %all-to-all-done = bf16[32,8,2048]{2,1,0:T(8,128)(2,1)S(1)} async-done(((bf16[32,8,2048]{2,1,0:T(8,128)(2,1)}), bf16[32,8,2048]{2,1,0:T(8,128)(2,1)S(1)}, u32[]{:S(2)}, u32[]{:S(2)}) %all-to-all-start) | async-done | bytes 1048608 | tf_op jit(solution)/shard_map/while/body/eval_jaxpr/all_to_all | solution.py:172
  219.2 25.2 %all-to-all-done.1 = bf16[32,8,2048]{2,1,0:T(8,128)(2,1)S(1)} async-done(((bf16[32,8,2048]{2,1,0:T(8,128)(2,1)}), bf16[32,8,2048]{2,1,0:T(8,128)(2,1)S(1)}, u32[]{:S(2)}, u32[]{:S(2)}) %all-to-all-start.1) | async-done | bytes 1048608 | tf_op jit(solution)/shard_map/while/body/eval_jaxpr/all_to_all | solution.py:175
  260.5 27.3 %all-to-all-done = bf16[32,8,2048]{2,1,0:T(8,128)(2,1)S(1)} async-done(((bf16[32,8,2048]{2,1,0:T(8,128)(2,1)}), bf16[32,8,2048]{2,1,0:T(8,128)(2,1)S(1)}, u32[]{:S(2)}, u32[]{:S(2)}) %all-to-all-start) | async-done | bytes 1048608 | tf_op jit(solution)/shard_map/while/body/eval_jaxpr/all_to_all | solution.py:172
  294.6 26.7 %all-to-all-done.1 = bf16[32,8,2048]{2,1,0:T(8,128)(2,1)S(1)} async-done(((bf16[32,8,2048]{2,1,0:T(8,128)(2,1)}), bf16[32,8,2048]{2,1,0:T(8,128)(2,1)S(1)}, u32[]{:S(2)}, u32[]{:S(2)}) %all-to-all-start.1) | async-done | bytes 1048608 | tf_op jit(solution)/shard_map/while/body/eval_jaxpr/all_to_all | solution.py:175
  323.6 11.2 %collective-permute-done = bf16[32,2048]{1,0:T(8,128)(2,1)S(1)} collective-permute-done((bf16[32,2048]{1,0:T(8,128)(2,1)S(1)}, bf16[32,2048]{1,0:T(8,128)(2,1)S(1)}, u32[]{:S(2)}, u32[]{:S(2)}) %collective-permute-start) | collective-permute-done | bytes 131104 | tf_op jit(solution)/shard_map/while/body/eval_jaxpr/ppermute | solution.py:13
  345.6 19.0 %all-to-all-done = bf16[32,8,2048]{2,1,0:T(8,128)(2,1)S(1)} async-done(((bf16[32,8,2048]{2,1,0:T(8,128)(2,1)}), bf16[32,8,2048]{2,1,0:T(8,128)(2,1)S(1)}, u32[]{:S(2)}, u32[]{:S(2)}) %all-to-all-start) | async-done | bytes 1048608 | tf_op jit(solution)/shard_map/while/body/eval_jaxpr/all_to_all | solution.py:172
  364.6 11.4 %conditional.4 = (bf16[256,2048]{1,0:T(8,128)(2,1)}) conditional(s32[]{:T(128)} %convert_element_type.170, () %tuple.60, (bf16[32,8,2048]{2,1,0:T(8,128)(2,1)S(1)}, bf16[2048,704]{1,0:T(8,128)(2,1)}, bf16[2048,704]{1,0:T(8,128)(2,1)}, bf16[704,2048]{1,0:T(8,128)(2,1)}) %tuple.61), branch_computations={%region_12.12_spmd, %region_13.13_spmd} | conditional | flops 2216198144 | bytes 13238280 | solution.py:174
  402.0 17.6 %collective-permute-done = bf16[32,2048]{1,0:T(8,128)(2,1)S(1)} collective-permute-done((bf16[32,2048]{1,0:T(8,128)(2,1)S(1)}, bf16[32,2048]{1,0:T(8,128)(2,1)S(1)}, u32[]{:S(2)}, u32[]{:S(2)}) %collective-permute-start) | collective-permute-done | bytes 131104 | tf_op jit(solution)/shard_map/while/body/eval_jaxpr/ppermute | solution.py:13
  430.4 18.2 %all-to-all-done = bf16[32,8,2048]{2,1,0:T(8,128)(2,1)S(1)} async-done(((bf16[32,8,2048]{2,1,0:T(8,128)(2,1)}), bf16[32,8,2048]{2,1,0:T(8,128)(2,1)S(1)}, u32[]{:S(2)}, u32[]{:S(2)}) %all-to-all-start) | async-done | bytes 1048608 | tf_op jit(solution)/shard_map/while/body/eval_jaxpr/all_to_all | solution.py:172
  448.6 11.4 %conditional.4 = (bf16[256,2048]{1,0:T(8,128)(2,1)}) conditional(s32[]{:T(128)} %convert_element_type.170, () %tuple.60, (bf16[32,8,2048]{2,1,0:T(8,128)(2,1)S(1)}, bf16[2048,704]{1,0:T(8,128)(2,1)}, bf16[2048,704]{1,0:T(8,128)(2,1)}, bf16[704,2048]{1,0:T(8,128)(2,1)}) %tuple.61), branch_computations={%region_12.12_spmd, %region_13.13_spmd} | conditional | flops 2216198144 | bytes 13238280 | solution.py:174
  486.0 18.4 %collective-permute-done = bf16[32,2048]{1,0:T(8,128)(2,1)S(1)} collective-permute-done((bf16[32,2048]{1,0:T(8,128)(2,1)S(1)}, bf16[32,2048]{1,0:T(8,128)(2,1)S(1)}, u32[]{:S(2)}, u32[]{:S(2)}) %collective-permute-start) | collective-permute-done | bytes 131104 | tf_op jit(solution)/shard_map/while/body/eval_jaxpr/ppermute | solution.py:13
  515.2 18.2 %all-to-all-done = bf16[32,8,2048]{2,1,0:T(8,128)(2,1)S(1)} async-done(((bf16[32,8,2048]{2,1,0:T(8,128)(2,1)}), bf16[32,8,2048]{2,1,0:T(8,128)(2,1)S(1)}, u32[]{:S(2)}, u32[]{:S(2)}) %all-to-all-start) | async-done | bytes 1048608 | tf_op jit(solution)/shard_map/while/body/eval_jaxpr/all_to_all | solution.py:172
  533.4 11.4 %conditional.4 = (bf16[256,2048]{1,0:T(8,128)(2,1)}) conditional(s32[]{:T(128)} %convert_element_type.170, () %tuple.60, (bf16[32,8,2048]{2,1,0:T(8,128)(2,1)S(1)}, bf16[2048,704]{1,0:T(8,128)(2,1)}, bf16[2048,704]{1,0:T(8,128)(2,1)}, bf16[704,2048]{1,0:T(8,128)(2,1)}) %tuple.61), branch_computations={%region_12.12_spmd, %region_13.13_spmd} | conditional | flops 2216198144 | bytes 13238280 | solution.py:174
  570.8 13.0 %collective-permute-done = bf16[32,2048]{1,0:T(8,128)(2,1)S(1)} collective-permute-done((bf16[32,2048]{1,0:T(8,128)(2,1)S(1)}, bf16[32,2048]{1,0:T(8,128)(2,1)S(1)}, u32[]{:S(2)}, u32[]{:S(2)}) %collective-permute-start) | collective-permute-done | bytes 131104 | tf_op jit(solution)/shard_map/while/body/eval_jaxpr/ppermute | solution.py:13
  593.5 18.2 %all-to-all-done = bf16[32,8,2048]{2,1,0:T(8,128)(2,1)S(1)} async-done(((bf16[32,8,2048]{2,1,0:T(8,128)(2,1)}), bf16[32,8,2048]{2,1,0:T(8,128)(2,1)S(1)}, u32[]{:S(2)}, u32[]{:S(2)}) %all-to-all-start) | async-done | bytes 1048608 | tf_op jit(solution)/shard_map/while/body/eval_jaxpr/all_to_all | solution.py:172
  611.7 11.4 %conditional.4 = (bf16[256,2048]{1,0:T(8,128)(2,1)}) conditional(s32[]{:T(128)} %convert_element_type.170, () %tuple.60, (bf16[32,8,2048]{2,1,0:T(8,128)(2,1)S(1)}, bf16[2048,704]{1,0:T(8,128)(2,1)}, bf16[2048,704]{1,0:T(8,128)(2,1)}, bf16[704,2048]{1,0:T(8,128)(2,1)}) %tuple.61), branch_computations={%region_12.12_spmd, %region_13.13_spmd} | conditional | flops 2216198144 | bytes 13238280 | solution.py:174
  668.4 19.5 %all-to-all-done = bf16[32,8,2048]{2,1,0:T(8,128)(2,1)S(1)} async-done(((bf16[32,8,2048]{2,1,0:T(8,128)(2,1)}), bf16[32,8,2048]{2,1,0:T(8,128)(2,1)S(1)}, u32[]{:S(2)}, u32[]{:S(2)}) %all-to-all-start) | async-done | bytes 1048608 | tf_op jit(solution)/shard_map/while/body/eval_jaxpr/all_to_all | solution.py:172
  695.1 28.7 %all-to-all-done.1 = bf16[32,8,2048]{2,1,0:T(8,128)(2,1)S(1)} async-done(((bf16[32,8,2048]{2,1,0:T(8,128)(2,1)}), bf16[32,8,2048]{2,1,0:T(8,128)(2,1)S(1)}, u32[]{:S(2)}, u32[]{:S(2)}) %all-to-all-start.1) | async-done | bytes 1048608 | tf_op jit(solution)/shard_map/while/body/eval_jaxpr/all_to_all | solution.py:175
  742.9 23.4 %all-to-all-done = bf16[32,8,2048]{2,1,0:T(8,128)(2,1)S(1)} async-done(((bf16[32,8,2048]{2,1,0:T(8,128)(2,1)}), bf16[32,8,2048]{2,1,0:T(8,128)(2,1)S(1)}, u32[]{:S(2)}, u32[]{:S(2)}) %all-to-all-start) | async-done | bytes 1048608 | tf_op jit(solution)/shard_map/while/body/eval_jaxpr/all_to_all | solution.py:172
  773.0 23.7 %all-to-all-done.1 = bf16[32,8,2048]{2,1,0:T(8,128)(2,1)S(1)} async-done(((bf16[32,8,2048]{2,1,0:T(8,128)(2,1)}), bf16[32,8,2048]{2,1,0:T(8,128)(2,1)S(1)}, u32[]{:S(2)}, u32[]{:S(2)}) %all-to-all-start.1) | async-done | bytes 1048608 | tf_op jit(solution)/shard_map/while/body/eval_jaxpr/all_to_all | solution.py:175
  817.5 22.2 %all-to-all-done = bf16[32,8,2048]{2,1,0:T(8,128)(2,1)S(1)} async-done(((bf16[32,8,2048]{2,1,0:T(8,128)(2,1)}), bf16[32,8,2048]{2,1,0:T(8,128)(2,1)S(1)}, u32[]{:S(2)}, u32[]{:S(2)}) %all-to-all-start) | async-done | bytes 1048608 | tf_op jit(solution)/shard_map/while/body/eval_jaxpr/all_to_all | solution.py:172
  846.3 22.3 %all-to-all-done.1 = bf16[32,8,2048]{2,1,0:T(8,128)(2,1)S(1)} async-done(((bf16[32,8,2048]{2,1,0:T(8,128)(2,1)}), bf16[32,8,2048]{2,1,0:T(8,128)(2,1)S(1)}, u32[]{:S(2)}, u32[]{:S(2)}) %all-to-all-start.1) | async-done | bytes 1048608 | tf_op jit(solution)/shard_map/while/body/eval_jaxpr/all_to_all | solution.py:175
  892.0 21.1 %all-to-all-done = bf16[32,8,2048]{2,1,0:T(8,128)(2,1)S(1)} async-done(((bf16[32,8,2048]{2,1,0:T(8,128)(2,1)}), bf16[32,8,2048]{2,1,0:T(8,128)(2,1)S(1)}, u32[]{:S(2)}, u32[]{:S(2)}) %all-to-all-start) | async-done | bytes 1048608 | tf_op jit(solution)/shard_map/while/body/eval_jaxpr/all_to_all | solution.py:172
  919.8 20.8 %all-to-all-done.1 = bf16[32,8,2048]{2,1,0:T(8,128)(2,1)S(1)} async-done(((bf16[32,8,2048]{2,1,0:T(8,128)(2,1)}), bf16[32,8,2048]{2,1,0:T(8,128)(2,1)S(1)}, u32[]{:S(2)}, u32[]{:S(2)}) %all-to-all-start.1) | async-done | bytes 1048608 | tf_op jit(solution)/shard_map/while/body/eval_jaxpr/all_to_all | solution.py:175
  942.8 13.0 %collective-permute-done = bf16[32,2048]{1,0:T(8,128)(2,1)S(1)} collective-permute-done((bf16[32,2048]{1,0:T(8,128)(2,1)S(1)}, bf16[32,2048]{1,0:T(8,128)(2,1)S(1)}, u32[]{:S(2)}, u32[]{:S(2)}) %collective-permute-start) | collective-permute-done | bytes 131104 | tf_op jit(solution)/shard_map/while/body/eval_jaxpr/ppermute | solution.py:13
  966.5 26.9 %all-to-all-done = bf16[32,8,2048]{2,1,0:T(8,128)(2,1)S(1)} async-done(((bf16[32,8,2048]{2,1,0:T(8,128)(2,1)}), bf16[32,8,2048]{2,1,0:T(8,128)(2,1)S(1)}, u32[]{:S(2)}, u32[]{:S(2)}) %all-to-all-start) | async-done | bytes 1048608 | tf_op jit(solution)/shard_map/while/body/eval_jaxpr/all_to_all | solution.py:172
  1000.1 26.4 %all-to-all-done.1 = bf16[32,8,2048]{2,1,0:T(8,128)(2,1)S(1)} async-done(((bf16[32,8,2048]{2,1,0:T(8,128)(2,1)}), bf16[32,8,2048]{2,1,0:T(8,128)(2,1)S(1)}, u32[]{:S(2)}, u32[]{:S(2)}) %all-to-all-start.1) | async-done | bytes 1048608 | tf_op jit(solution)/shard_map/while/body/eval_jaxpr/all_to_all | solution.py:175
  (389 shorter events, 420.2 us)
Async XLA Ops:
  6.5 88.1 %all-gather.3.cloned.1.call-start = ((), (), s32[]{:S(2)}) async-start(), calls=%async_computation.3 | async-start | bytes 4325376 | tf_op jit(solution)/shard_map/all_gather | solution.py:78
  7.3 168.6 %all-gather.5.cloned.1.call-start = ((), (), s32[]{:S(2)}) async-start(), calls=%async_computation.4 | async-start | bytes 4325376 | tf_op jit(solution)/shard_map/all_gather | solution.py:81
  9.6 69.5 %all-to-all-start.2 = ((bf16[32,1,64,128]{3,2,1,0:T(8,128)(2,1)}), bf16[32,1,64,128]{3,2,1,0:T(8,128)(2,1)S(1)}, u32[]{:S(2)}, u32[]{:S(2)}) async-start(bf16[32,1,64,128]{3,2,1,0:T(8,128)(2,1)} %stack.2), calls=%async_computation.2 | async-start | bytes 1048576 | tf_op jit(solution)/shard_map/all_to_all | solution.py:73
  180.0 32.4 %all-to-all-start = ((bf16[32,8,2048]{2,1,0:T(8,128)(2,1)}), bf16[32,8,2048]{2,1,0:T(8,128)(2,1)S(1)}, u32[]{:S(2)}, u32[]{:S(2)}) async-start(bf16[32,8,2048]{2,1,0:T(8,128)(2,1)} %fusion.71), calls=%async_computation | async-start | bytes 2097152 | tf_op jit(solution)/shard_map/while/body/eval_jaxpr/all_to_all | solution.py:172
  213.5 30.8 %all-to-all-start.1 = ((bf16[32,8,2048]{2,1,0:T(8,128)(2,1)}), bf16[32,8,2048]{2,1,0:T(8,128)(2,1)S(1)}, u32[]{:S(2)}, u32[]{:S(2)}) async-start(bf16[32,8,2048]{2,1,0:T(8,128)(2,1)} %bitcast.126), calls=%async_computation.1 | async-start | bytes 2097152 | tf_op jit(solution)/shard_map/while/body/eval_jaxpr/all_to_all | solution.py:175
  255.0 32.9 %all-to-all-start = ((bf16[32,8,2048]{2,1,0:T(8,128)(2,1)}), bf16[32,8,2048]{2,1,0:T(8,128)(2,1)S(1)}, u32[]{:S(2)}, u32[]{:S(2)}) async-start(bf16[32,8,2048]{2,1,0:T(8,128)(2,1)} %fusion.71), calls=%async_computation | async-start | bytes 2097152 | tf_op jit(solution)/shard_map/while/body/eval_jaxpr/all_to_all | solution.py:172
  289.0 32.4 %all-to-all-start.1 = ((bf16[32,8,2048]{2,1,0:T(8,128)(2,1)}), bf16[32,8,2048]{2,1,0:T(8,128)(2,1)S(1)}, u32[]{:S(2)}, u32[]{:S(2)}) async-start(bf16[32,8,2048]{2,1,0:T(8,128)(2,1)} %bitcast.126), calls=%async_computation.1 | async-start | bytes 2097152 | tf_op jit(solution)/shard_map/while/body/eval_jaxpr/all_to_all | solution.py:175
  321.7 13.1 %collective-permute-start = (bf16[32,2048]{1,0:T(8,128)(2,1)S(1)}, bf16[32,2048]{1,0:T(8,128)(2,1)S(1)}, u32[]{:S(2)}, u32[]{:S(2)}) collective-permute-start(bf16[32,2048]{1,0:T(8,128)(2,1)S(1)} %get-tuple-element.610), channel_id=1, source_target_pairs={{0,32},{32,64},{64,96},{96,128},{128,160},{160,192},{192,224},{1,3... | collective-permute-start | bytes 393224 | tf_op jit(solution)/shard_map/while/body/eval_jaxpr/ppermute | solution.py:13
  338.9 25.7 %all-to-all-start = ((bf16[32,8,2048]{2,1,0:T(8,128)(2,1)}), bf16[32,8,2048]{2,1,0:T(8,128)(2,1)S(1)}, u32[]{:S(2)}, u32[]{:S(2)}) async-start(bf16[32,8,2048]{2,1,0:T(8,128)(2,1)} %fusion.71), calls=%async_computation | async-start | bytes 2097152 | tf_op jit(solution)/shard_map/while/body/eval_jaxpr/all_to_all | solution.py:172
  375.9 23.8 %all-to-all-start.1 = ((bf16[32,8,2048]{2,1,0:T(8,128)(2,1)}), bf16[32,8,2048]{2,1,0:T(8,128)(2,1)S(1)}, u32[]{:S(2)}, u32[]{:S(2)}) async-start(bf16[32,8,2048]{2,1,0:T(8,128)(2,1)} %bitcast.126), calls=%async_computation.1 | async-start | bytes 2097152 | tf_op jit(solution)/shard_map/while/body/eval_jaxpr/all_to_all | solution.py:175
  400.1 19.6 %collective-permute-start = (bf16[32,2048]{1,0:T(8,128)(2,1)S(1)}, bf16[32,2048]{1,0:T(8,128)(2,1)S(1)}, u32[]{:S(2)}, u32[]{:S(2)}) collective-permute-start(bf16[32,2048]{1,0:T(8,128)(2,1)S(1)} %get-tuple-element.610), channel_id=1, source_target_pairs={{0,32},{32,64},{64,96},{96,128},{128,160},{160,192},{192,224},{1,3... | collective-permute-start | bytes 393224 | tf_op jit(solution)/shard_map/while/body/eval_jaxpr/ppermute | solution.py:13
  423.7 24.9 %all-to-all-start = ((bf16[32,8,2048]{2,1,0:T(8,128)(2,1)}), bf16[32,8,2048]{2,1,0:T(8,128)(2,1)S(1)}, u32[]{:S(2)}, u32[]{:S(2)}) async-start(bf16[32,8,2048]{2,1,0:T(8,128)(2,1)} %fusion.71), calls=%async_computation | async-start | bytes 2097152 | tf_op jit(solution)/shard_map/while/body/eval_jaxpr/all_to_all | solution.py:172
  460.0 23.8 %all-to-all-start.1 = ((bf16[32,8,2048]{2,1,0:T(8,128)(2,1)}), bf16[32,8,2048]{2,1,0:T(8,128)(2,1)S(1)}, u32[]{:S(2)}, u32[]{:S(2)}) async-start(bf16[32,8,2048]{2,1,0:T(8,128)(2,1)} %bitcast.126), calls=%async_computation.1 | async-start | bytes 2097152 | tf_op jit(solution)/shard_map/while/body/eval_jaxpr/all_to_all | solution.py:175
  484.1 20.3 %collective-permute-start = (bf16[32,2048]{1,0:T(8,128)(2,1)S(1)}, bf16[32,2048]{1,0:T(8,128)(2,1)S(1)}, u32[]{:S(2)}, u32[]{:S(2)}) collective-permute-start(bf16[32,2048]{1,0:T(8,128)(2,1)S(1)} %get-tuple-element.610), channel_id=1, source_target_pairs={{0,32},{32,64},{64,96},{96,128},{128,160},{160,192},{192,224},{1,3... | collective-permute-start | bytes 393224 | tf_op jit(solution)/shard_map/while/body/eval_jaxpr/ppermute | solution.py:13
  508.5 24.9 %all-to-all-start = ((bf16[32,8,2048]{2,1,0:T(8,128)(2,1)}), bf16[32,8,2048]{2,1,0:T(8,128)(2,1)S(1)}, u32[]{:S(2)}, u32[]{:S(2)}) async-start(bf16[32,8,2048]{2,1,0:T(8,128)(2,1)} %fusion.71), calls=%async_computation | async-start | bytes 2097152 | tf_op jit(solution)/shard_map/while/body/eval_jaxpr/all_to_all | solution.py:172
  544.8 23.8 %all-to-all-start.1 = ((bf16[32,8,2048]{2,1,0:T(8,128)(2,1)}), bf16[32,8,2048]{2,1,0:T(8,128)(2,1)S(1)}, u32[]{:S(2)}, u32[]{:S(2)}) async-start(bf16[32,8,2048]{2,1,0:T(8,128)(2,1)} %bitcast.126), calls=%async_computation.1 | async-start | bytes 2097152 | tf_op jit(solution)/shard_map/while/body/eval_jaxpr/all_to_all | solution.py:175
  568.9 14.9 %collective-permute-start = (bf16[32,2048]{1,0:T(8,128)(2,1)S(1)}, bf16[32,2048]{1,0:T(8,128)(2,1)S(1)}, u32[]{:S(2)}, u32[]{:S(2)}) collective-permute-start(bf16[32,2048]{1,0:T(8,128)(2,1)S(1)} %get-tuple-element.610), channel_id=1, source_target_pairs={{0,32},{32,64},{64,96},{96,128},{128,160},{160,192},{192,224},{1,3... | collective-permute-start | bytes 393224 | tf_op jit(solution)/shard_map/while/body/eval_jaxpr/ppermute | solution.py:13
  587.9 23.8 %all-to-all-start = ((bf16[32,8,2048]{2,1,0:T(8,128)(2,1)}), bf16[32,8,2048]{2,1,0:T(8,128)(2,1)S(1)}, u32[]{:S(2)}, u32[]{:S(2)}) async-start(bf16[32,8,2048]{2,1,0:T(8,128)(2,1)} %fusion.71), calls=%async_computation | async-start | bytes 2097152 | tf_op jit(solution)/shard_map/while/body/eval_jaxpr/all_to_all | solution.py:172
  623.1 23.8 %all-to-all-start.1 = ((bf16[32,8,2048]{2,1,0:T(8,128)(2,1)}), bf16[32,8,2048]{2,1,0:T(8,128)(2,1)S(1)}, u32[]{:S(2)}, u32[]{:S(2)}) async-start(bf16[32,8,2048]{2,1,0:T(8,128)(2,1)} %bitcast.126), calls=%async_computation.1 | async-start | bytes 2097152 | tf_op jit(solution)/shard_map/while/body/eval_jaxpr/all_to_all | solution.py:175
  647.2 10.7 %collective-permute-start = (bf16[32,2048]{1,0:T(8,128)(2,1)S(1)}, bf16[32,2048]{1,0:T(8,128)(2,1)S(1)}, u32[]{:S(2)}, u32[]{:S(2)}) collective-permute-start(bf16[32,2048]{1,0:T(8,128)(2,1)S(1)} %get-tuple-element.610), channel_id=1, source_target_pairs={{0,32},{32,64},{64,96},{96,128},{128,160},{160,192},{192,224},{1,3... | collective-permute-start | bytes 393224 | tf_op jit(solution)/shard_map/while/body/eval_jaxpr/ppermute | solution.py:13
  662.0 26.0 %all-to-all-start = ((bf16[32,8,2048]{2,1,0:T(8,128)(2,1)}), bf16[32,8,2048]{2,1,0:T(8,128)(2,1)S(1)}, u32[]{:S(2)}, u32[]{:S(2)}) async-start(bf16[32,8,2048]{2,1,0:T(8,128)(2,1)} %fusion.71), calls=%async_computation | async-start | bytes 2097152 | tf_op jit(solution)/shard_map/while/body/eval_jaxpr/all_to_all | solution.py:172
  689.1 34.7 %all-to-all-start.1 = ((bf16[32,8,2048]{2,1,0:T(8,128)(2,1)}), bf16[32,8,2048]{2,1,0:T(8,128)(2,1)S(1)}, u32[]{:S(2)}, u32[]{:S(2)}) async-start(bf16[32,8,2048]{2,1,0:T(8,128)(2,1)} %bitcast.126), calls=%async_computation.1 | async-start | bytes 2097152 | tf_op jit(solution)/shard_map/while/body/eval_jaxpr/all_to_all | solution.py:175
  736.2 30.1 %all-to-all-start = ((bf16[32,8,2048]{2,1,0:T(8,128)(2,1)}), bf16[32,8,2048]{2,1,0:T(8,128)(2,1)S(1)}, u32[]{:S(2)}, u32[]{:S(2)}) async-start(bf16[32,8,2048]{2,1,0:T(8,128)(2,1)} %fusion.71), calls=%async_computation | async-start | bytes 2097152 | tf_op jit(solution)/shard_map/while/body/eval_jaxpr/all_to_all | solution.py:172
  767.4 29.4 %all-to-all-start.1 = ((bf16[32,8,2048]{2,1,0:T(8,128)(2,1)}), bf16[32,8,2048]{2,1,0:T(8,128)(2,1)S(1)}, u32[]{:S(2)}, u32[]{:S(2)}) async-start(bf16[32,8,2048]{2,1,0:T(8,128)(2,1)} %bitcast.126), calls=%async_computation.1 | async-start | bytes 2097152 | tf_op jit(solution)/shard_map/while/body/eval_jaxpr/all_to_all | solution.py:175
  810.8 28.9 %all-to-all-start = ((bf16[32,8,2048]{2,1,0:T(8,128)(2,1)}), bf16[32,8,2048]{2,1,0:T(8,128)(2,1)S(1)}, u32[]{:S(2)}, u32[]{:S(2)}) async-start(bf16[32,8,2048]{2,1,0:T(8,128)(2,1)} %fusion.71), calls=%async_computation | async-start | bytes 2097152 | tf_op jit(solution)/shard_map/while/body/eval_jaxpr/all_to_all | solution.py:172
  840.7 27.9 %all-to-all-start.1 = ((bf16[32,8,2048]{2,1,0:T(8,128)(2,1)}), bf16[32,8,2048]{2,1,0:T(8,128)(2,1)S(1)}, u32[]{:S(2)}, u32[]{:S(2)}) async-start(bf16[32,8,2048]{2,1,0:T(8,128)(2,1)} %bitcast.126), calls=%async_computation.1 | async-start | bytes 2097152 | tf_op jit(solution)/shard_map/while/body/eval_jaxpr/all_to_all | solution.py:175
  868.9 12.3 %collective-permute-start = (bf16[32,2048]{1,0:T(8,128)(2,1)S(1)}, bf16[32,2048]{1,0:T(8,128)(2,1)S(1)}, u32[]{:S(2)}, u32[]{:S(2)}) collective-permute-start(bf16[32,2048]{1,0:T(8,128)(2,1)S(1)} %get-tuple-element.610), channel_id=1, source_target_pairs={{0,32},{32,64},{64,96},{96,128},{128,160},{160,192},{192,224},{1,3... | collective-permute-start | bytes 393224 | tf_op jit(solution)/shard_map/while/body/eval_jaxpr/ppermute | solution.py:13
  885.3 27.8 %all-to-all-start = ((bf16[32,8,2048]{2,1,0:T(8,128)(2,1)}), bf16[32,8,2048]{2,1,0:T(8,128)(2,1)S(1)}, u32[]{:S(2)}, u32[]{:S(2)}) async-start(bf16[32,8,2048]{2,1,0:T(8,128)(2,1)} %fusion.71), calls=%async_computation | async-start | bytes 2097152 | tf_op jit(solution)/shard_map/while/body/eval_jaxpr/all_to_all | solution.py:172
  914.2 26.4 %all-to-all-start.1 = ((bf16[32,8,2048]{2,1,0:T(8,128)(2,1)}), bf16[32,8,2048]{2,1,0:T(8,128)(2,1)S(1)}, u32[]{:S(2)}, u32[]{:S(2)}) async-start(bf16[32,8,2048]{2,1,0:T(8,128)(2,1)} %bitcast.126), calls=%async_computation.1 | async-start | bytes 2097152 | tf_op jit(solution)/shard_map/while/body/eval_jaxpr/all_to_all | solution.py:175
  940.9 14.9 %collective-permute-start = (bf16[32,2048]{1,0:T(8,128)(2,1)S(1)}, bf16[32,2048]{1,0:T(8,128)(2,1)S(1)}, u32[]{:S(2)}, u32[]{:S(2)}) collective-permute-start(bf16[32,2048]{1,0:T(8,128)(2,1)S(1)} %get-tuple-element.610), channel_id=1, source_target_pairs={{0,32},{32,64},{64,96},{96,128},{128,160},{160,192},{192,224},{1,3... | collective-permute-start | bytes 393224 | tf_op jit(solution)/shard_map/while/body/eval_jaxpr/ppermute | solution.py:13
  959.9 33.5 %all-to-all-start = ((bf16[32,8,2048]{2,1,0:T(8,128)(2,1)}), bf16[32,8,2048]{2,1,0:T(8,128)(2,1)S(1)}, u32[]{:S(2)}, u32[]{:S(2)}) async-start(bf16[32,8,2048]{2,1,0:T(8,128)(2,1)} %fusion.71), calls=%async_computation | async-start | bytes 2097152 | tf_op jit(solution)/shard_map/while/body/eval_jaxpr/all_to_all | solution.py:172
  994.5 32.1 %all-to-all-start.1 = ((bf16[32,8,2048]{2,1,0:T(8,128)(2,1)}), bf16[32,8,2048]{2,1,0:T(8,128)(2,1)S(1)}, u32[]{:S(2)}, u32[]{:S(2)}) async-start(bf16[32,8,2048]{2,1,0:T(8,128)(2,1)} %bitcast.126), calls=%async_computation.1 | async-start | bytes 2097152 | tf_op jit(solution)/shard_map/while/body/eval_jaxpr/all_to_all | solution.py:175
  (11 other events, 444.0 us)
Sparse Core Ops, SparseCore 0:
  9.9 84.7 all-gather.2
  97.2 78.5 all-gather.4
